TPU v7x, 32 devices: a whole 2x2x4 slice. The times are simulated.
32 devices in a mesh: blk: 32 (over z, y, x, core).
Axes of the slice: x: 2, y: 2, z: 4, core: 2. Of those that a mesh axis runs over, the one named last changes fastest.
Arguments:
- adjacency: int32 [8192, 1280], P('blk'), may hold values 0 or 1
- weight: bfloat16 [8192, 1280], P('blk'), may hold values from -6 to 6
Outputs:
- closure: float32 [8192, 4352], P('blk')
All inputs are finite; a program needn't handle non-finite values. No bound on the sum of `adjacency` on one device may be relied on, other than what follows from the above.
Results may differ from a plain program's by a relative error of at most 0.0041.
Values may be sent and summed in bfloat16 or wider, within the bound.
A program may use at most 64 MiB of HBM per device.

v0:
```python
import functools
import math

import jax
import jax.numpy as jnp
from jax import lax
from jax.experimental import pallas as pl
from jax.experimental.pallas import tpu as pltpu
from jax.sharding import PartitionSpec as P

B = 512
MESH = pl.DeviceIdType.MESH
CORES = 2
PLANE = 4
SPAN = PLANE - 1
PAD = 16
CHUNKS = 4


def banded(adjacency, weight):
    row_count = adjacency.shape[0]
    reach = (adjacency.shape[1] // row_count - 1) // 2
    local_row = lax.broadcasted_iota(jnp.int32, adjacency.shape, 0)
    offset = lax.broadcasted_iota(jnp.int32, adjacency.shape, 1) - local_row - reach * row_count
    keep = (jnp.abs(offset) <= B) & ((adjacency == 1) | (offset == 0))
    return jnp.where(keep, weight, jnp.zeros_like(weight))


def pack(matrix):
    rows = matrix.shape[0]
    first, last = matrix[:, :rows], matrix[:, -rows:]
    r = lax.broadcasted_iota(jnp.int32, (rows, rows), 0)
    c = lax.broadcasted_iota(jnp.int32, (rows, rows), 1)
    square = jnp.where(c >= r, first, last)
    diagonal = jnp.sum(jnp.where(c == r, last, 0).astype(jnp.float32), axis=0, keepdims=True)
    diagonal = jnp.pad(diagonal.astype(matrix.dtype), ((0, PAD - 1), (0, matrix.shape[1] - 2 * rows)))
    body = jnp.concatenate([square, matrix[:, rows:-rows]], axis=1)
    return jnp.concatenate([body, diagonal], axis=0)


def kernel(
    n, rows, packed, out, buf, cols, row, p_low, t_low,
    own_send, pair_send, hop_send, side_send, recv, local_sem,
):
    me = lax.axis_index("blk")
    core = me % CORES
    place = (me // CORES) % PLANE
    group = me // (CORES * PLANE)
    groups = n // (CORES * PLANE)
    partner = me + 1 - 2 * core
    up = ((group + 1) % groups * PLANE + place) * CORES + core
    down = ((group + groups - 1) % groups * PLANE + place) * CORES + core
    x_mate = place + 1 - 2 * (place % 2)
    y_mate = (place + 2) % PLANE
    inner = (place + 1) // 2 % 2
    a_mate = (1 - inner) * x_mate + inner * y_mate
    b_mate = inner * x_mate + (1 - inner) * y_mate
    d_mate = SPAN - place

    def device(q):
        return (group * PLANE + q) * CORES + core

    def slot(chip_offset, c):
        return (chip_offset + SPAN) * CORES + c

    def is_above(q, p):
        return (q - p + PLANE) // PLANE

    def cross(q, p):
        return q - p + PLANE - 2 * PLANE * is_above(q, p)

    total = rows + PAD
    step = rows // CHUNKS
    bounds = [(j * step, step if j < CHUNKS - 1 else total - j * step) for j in range(CHUNKS)]

    barrier = pltpu.get_barrier_semaphore()
    greeted = [partner, up, down, device(a_mate), device(b_mate)]
    for other in greeted:
        pl.semaphore_signal(barrier, inc=1, device_id=(other,), device_id_type=MESH)
    pl.semaphore_wait(barrier, len(greeted))

    def chunk(ref, j):
        return ref.at[pl.ds(bounds[j][0], bounds[j][1])]

    sent = []

    def send(source, sem, j, to, at):
        copy = pltpu.make_async_remote_copy(
            src_ref=chunk(source, j),
            dst_ref=chunk(buf.at[at], j),
            send_sem=sem,
            recv_sem=recv.at[at, j],
            device_id=(to,),
            device_id_type=MESH,
        )
        copy.start()
        sent.append(copy)

    def arrived(at, j):
        pltpu.make_async_copy(chunk(packed, j), chunk(buf.at[at], j), recv.at[at, j]).wait()

    def pair(index, at, j):
        send(buf.at[at], pair_send.at[index, j], j, partner, at)

    def hop(index, q, j):
        above = is_above(q, place)
        to = above * up + (1 - above) * down
        send(buf.at[slot(q - place, core)], hop_send.at[index, j], j, to, slot(cross(q, place), core))

    center = slot(0, core)
    a_in, b_in, d_in = (slot(q - place, core) for q in (a_mate, b_mate, d_mate))
    a_far, b_far, d_far = (slot(cross(q, place), core) for q in (a_mate, b_mate, d_mate))

    for j in range(CHUNKS):
        send(packed, own_send.at[0, j], j, device(b_mate), slot(place - b_mate, core))
        send(packed, own_send.at[1, j], j, device(a_mate), slot(place - a_mate, core))
    mine = pltpu.make_async_copy(packed, buf.at[center], local_sem)
    mine.start()
    for j in range(CHUNKS):
        send(packed, own_send.at[2, j], j, partner, center)

    r = lax.broadcasted_iota(jnp.int32, (rows, rows), 0)
    c = lax.broadcasted_iota(jnp.int32, (rows, rows), 1)

    def triangles(at):
        square = buf[at, :rows, :rows]
        diagonal = buf[at, rows : rows + 1, :rows]
        zero = jnp.zeros_like(square)
        return (
            jnp.where(c >= r, square, zero),
            jnp.where(c < r, square, jnp.where(c == r, diagonal, zero)),
        )

    def unpack(at):
        first, last = triangles(at)
        cols[at, 4 * rows : 5 * rows, :] = first
        for k in range(1, 4):
            cols[at + k, (4 - k) * rows : (5 - k) * rows, :] = buf[at, :rows, k * rows : (k + 1) * rows]
        cols[at + 4, :rows, :] = last

    def take_other(at):
        other = at + 1 - 2 * core
        for j in range(CHUNKS):
            arrived(other, j)
        unpack(other)

    for j in range(CHUNKS):
        arrived(b_in, j)
        hop(0, b_mate, j)
        pair(0, b_in, j)
        arrived(a_in, j)
        send(buf.at[a_in], side_send.at[0, j], j, device(b_mate), slot(a_mate - b_mate, core))
        pair(1, a_in, j)
    for j in range(CHUNKS):
        hop(1, a_mate, j)
    for j in range(CHUNKS):
        arrived(b_far, j)
        send(
            buf.at[b_far], side_send.at[1, j], j, device(a_mate),
            slot(cross(b_mate, place) + place - a_mate, core),
        )
        pair(2, b_far, j)
    mine.wait()
    first, last = triangles(center)
    row[:, :rows] = first
    row[:, rows : 4 * rows] = buf[center, :rows, rows:]
    row[:, 4 * rows :] = last
    for at in (center, a_in, b_in, b_far):
        unpack(at)
    for at in (center, a_in, b_in):
        take_other(at)
    for j in range(CHUNKS):
        arrived(d_in, j)
        pair(3, d_in, j)
        arrived(a_far, j)
        pair(4, a_far, j)
        arrived(d_far, j)
        pair(5, d_far, j)
    for at in (d_in, a_far, d_far):
        unpack(at)
    for at in (b_far, d_in, a_far, d_far):
        take_other(at)

    def product(left, least, most, column):
        low, high = max(least, column - 4), min(most, column)
        return jnp.dot(
            left[:, (low - least) * rows : (high + 1 - least) * rows],
            cols[column + core, (low - column + 4) * rows : (high - column + 5) * rows, :],
            preferred_element_type=jnp.float32,
        )

    for u in range(9):
        p_low[:, u * rows : (u + 1) * rows] = (
            product(row, 4, 8, u + 4) * (1.0 / math.sqrt(B))
        ).astype(p_low.dtype)
    scale = 1.0 / math.sqrt(B) / math.sqrt(2 * B)
    for u in range(13):
        t_low[:, u * rows : (u + 1) * rows] = (product(p_low, 2, 10, u + 2) * scale).astype(t_low.dtype)
    for u in range(17):
        out[:, u * rows : (u + 1) * rows] = product(t_low, 0, 12, u)
    for copy in sent:
        copy.wait_send()


def local(n, adjacency, weight):
    rows = adjacency.shape[0]
    packed = pack(banded(adjacency, weight))
    wide = packed.shape[1]
    slots = (2 * SPAN + 1) * CORES
    low = packed.dtype
    return pl.pallas_call(
        functools.partial(kernel, n, rows),
        out_shape=jax.ShapeDtypeStruct((rows, 17 * rows), jnp.float32),
        in_specs=[pl.BlockSpec(memory_space=pltpu.VMEM)],
        out_specs=pl.BlockSpec(memory_space=pltpu.VMEM),
        scratch_shapes=[
            pltpu.VMEM((slots, rows + PAD, wide), low),
            pltpu.VMEM((slots + 4, 5 * rows, rows), low),
            pltpu.VMEM((rows, 5 * rows), low),
            pltpu.VMEM((rows, 9 * rows), low),
            pltpu.VMEM((rows, 13 * rows), low),
            pltpu.SemaphoreType.DMA((3, CHUNKS)),
            pltpu.SemaphoreType.DMA((6, CHUNKS)),
            pltpu.SemaphoreType.DMA((2, CHUNKS)),
            pltpu.SemaphoreType.DMA((2, CHUNKS)),
            pltpu.SemaphoreType.DMA((slots, CHUNKS)),
            pltpu.SemaphoreType.DMA,
        ],
        compiler_params=pltpu.CompilerParams(
            collective_id=0, has_side_effects=True, vmem_limit_bytes=40 * 1024 * 1024
        ),
    )(packed)


def solution(mesh):
    in_specs = (P("blk", None), P("blk", None))
    out_specs = P("blk", None)
    n = mesh.shape["blk"]
    return jax.shard_map(
        functools.partial(local, n), mesh=mesh, in_specs=in_specs, out_specs=out_specs, check_vma=False
    )
```

profile of v0, /device:TPU:1, one launch (start us, length us, event | category | flops | bytes accessed | tf_op | source)
XLA Modules:
  0.0 47.7 jit_solution(1203398695016226088)
XLA Ops:
  0.0 1.9 %fusion.3 = bf16[256,1280]{1,0:T(8,128)(2,1)S(1)} fusion(bf16[256,1280]{1,0:T(8,128)(2,1)} %param.3, s32[256,1280]{1,0:T(8,128)} %param.2), kind=kLoop, calls=%fused_computation.5 | loop fusion | flops 2949120 | bytes 2621440 | tf_op jit(solution)/shard_map/jit(_where)/select_n | solution.py:26
  1.9 0.1 fusion.6
  2.0 0.1 fusion.5.packed
  2.0 43.5 %shard_map.28 = f32[256,4352]{1,0:T(8,128)S(1)} custom-call(bf16[272,1024]{1,0:T(8,128)(2,1)S(1)} %fusion.5.packed), custom_call_target="tpu_custom_call" | custom-call | tf_op jit(solution)/shard_map/pallas_call | solution.py:211
  45.6 2.1 %copy.4 = f32[256,4352]{1,0:T(8,128)} copy(f32[256,4352]{1,0:T(8,128)S(1)} %shard_map.28) | data formatting | bytes 8912896
  (2 shorter events, 0.0 us)
where the time goes:
time: 47.8 us; the launch traced here: 47.7 us
  Pallas kernels  43.5 us (91%)
  local copies, waits for them, and re-layouts  2.13 us (4%)
  other arithmetic  1.99 us (4%)
    pallas_call x1, Pallas kernels, local(): pl.pallas_call(functools.partial(kernel, n, rows), out_shape=jax.ShapeDty...  43.5 us
    unnamed x1, local copies, waits for them, and re-layouts  2.1 us
    select_n x1, other arithmetic, banded(): return jnp.where(keep, weight, jnp.zeros_like(weight))  1.87 us

commit v1 on v0

v1 whole, which is shorter than its diff:
```python
import functools
import math

import jax
import jax.numpy as jnp
from jax import lax
from jax.experimental import pallas as pl
from jax.experimental.pallas import tpu as pltpu
from jax.sharding import PartitionSpec as P

B = 512
MESH = pl.DeviceIdType.MESH
CORES = 2
PLANE = 4
SPAN = PLANE - 1
LANES = 128
PAD = 16
CUTS = (128, 256, 512, 768, 1024, 1280, 1536, 1792)
ENDS = (4, 8, 12, 15, 16)


def block_of(buf, tri, at, k, rows):
    if k in (0, 4):
        return tri[at, k // 4]
    low = 2 * k * rows
    return jnp.concatenate([buf[at, low : low + rows, :], buf[at, low + rows : low + 2 * rows, :]], axis=1)


def product(left, buf, tri, core, rows, reach, u):
    low, high = max(-reach, u - 2), min(reach, u + 2)
    right = jnp.concatenate(
        [block_of(buf, tri, m + 2 * SPAN + core, u - m + 2, rows) for m in range(low, high + 1)], axis=0
    )
    return jnp.dot(
        left[:, (low + reach) * rows : (high + reach + 1) * rows], right, preferred_element_type=jnp.float32
    )


def gather_kernel(
    n, rows, adjacency, weight, t_low, buf, tri, adj, wgt, row, p_low,
    own_send, pair_send, hop_send, side_send, recv, in_sem,
):
    me = lax.axis_index("blk")
    core = me % CORES
    place = (me // CORES) % PLANE
    group = me // (CORES * PLANE)
    groups = n // (CORES * PLANE)
    partner = me + 1 - 2 * core
    up = ((group + 1) % groups * PLANE + place) * CORES + core
    down = ((group + groups - 1) % groups * PLANE + place) * CORES + core
    x_mate = place + 1 - 2 * (place % 2)
    y_mate = (place + 2) % PLANE
    inner = (place + 1) // 2 % 2
    a_mate = (1 - inner) * x_mate + inner * y_mate
    b_mate = inner * x_mate + (1 - inner) * y_mate
    d_mate = SPAN - place

    def device(q):
        return (group * PLANE + q) * CORES + core

    def slot(chip_offset, c):
        return (chip_offset + SPAN) * CORES + c

    def is_above(q, p):
        return (q - p + PLANE) // PLANE

    def cross(q, p):
        return q - p + PLANE - 2 * PLANE * is_above(q, p)

    total = buf.shape[1]
    starts = (0,) + CUTS
    ends = CUTS + (total,)
    chunks = len(starts)
    bounds = [(s, e - s) for s, e in zip(starts, ends)]

    barrier = pltpu.get_barrier_semaphore()
    greeted = [partner, up, down, device(a_mate), device(b_mate)]
    for other in greeted:
        pl.semaphore_signal(barrier, inc=1, device_id=(other,), device_id_type=MESH)

    order = (1, 2, 3, 0, 4)
    loads = []
    for k in order:
        cols = pl.ds(k * rows, rows)
        pair_of = (
            pltpu.make_async_copy(adjacency.at[:, cols], adj.at[:, cols], in_sem.at[0, k]),
            pltpu.make_async_copy(weight.at[:, cols], wgt.at[:, cols], in_sem.at[1, k]),
        )
        for load in pair_of:
            load.start()
        loads.append(pair_of)

    center = slot(0, core)
    r = lax.broadcasted_iota(jnp.int32, (rows, rows), 0)
    c = lax.broadcasted_iota(jnp.int32, (rows, rows), 1)
    for k, pair_of in zip(order, loads):
        for load in pair_of:
            load.wait()
        cols = slice(k * rows, (k + 1) * rows)
        offset = c - r + (k - 2) * rows
        keep = (adj[:, cols] == 1) | (offset == 0)
        if k in (0, 4):
            keep &= jnp.abs(offset) <= B
        kept = jnp.where(keep, wgt[:, cols].astype(jnp.float32), 0.0)
        low = kept.astype(row.dtype)
        row[:, cols] = low
        if k in (1, 2, 3):
            buf[center, 2 * k * rows : (2 * k + 1) * rows, :] = low[:, :LANES]
            buf[center, (2 * k + 1) * rows : (2 * k + 2) * rows, :] = low[:, LANES:]
        elif k == 0:
            first = kept
        else:
            square = jnp.where(c >= r, first, kept).astype(row.dtype)
            buf[center, :rows, :] = square[:, :LANES]
            buf[center, rows : 2 * rows, :] = square[:, LANES:]
            diagonal = jnp.sum(jnp.where(c == r, kept, 0.0), axis=0, keepdims=True)
            tail = jnp.concatenate(
                [diagonal[:, :LANES], diagonal[:, LANES:], jnp.zeros((PAD - 2, LANES), jnp.float32)], axis=0
            )
            buf[center, 8 * rows :, :] = tail.astype(row.dtype)
    pl.semaphore_wait(barrier, len(greeted))

    def chunk(ref, j):
        return ref.at[pl.ds(bounds[j][0], bounds[j][1])]

    sent = []

    def send(source, sem, j, to, at):
        copy = pltpu.make_async_remote_copy(
            src_ref=chunk(source, j),
            dst_ref=chunk(buf.at[at], j),
            send_sem=sem,
            recv_sem=recv.at[at, j],
            device_id=(to,),
            device_id_type=MESH,
        )
        copy.start()
        sent.append(copy)

    def arrived(at, j):
        pltpu.make_async_copy(chunk(buf.at[center], j), chunk(buf.at[at], j), recv.at[at, j]).wait()

    def pair(index, at, j):
        send(buf.at[at], pair_send.at[index, j], j, partner, at)

    def hop(index, q, j):
        above = is_above(q, place)
        to = above * up + (1 - above) * down
        send(buf.at[slot(q - place, core)], hop_send.at[index, j], j, to, slot(cross(q, place), core))

    a_in, b_in, d_in = (slot(q - place, core) for q in (a_mate, b_mate, d_mate))
    a_far, b_far, d_far = (slot(cross(q, place), core) for q in (a_mate, b_mate, d_mate))

    mine = buf.at[center]
    for j in range(chunks):
        send(mine, own_send.at[0, j], j, device(b_mate), slot(place - b_mate, core))
        send(mine, own_send.at[1, j], j, device(a_mate), slot(place - a_mate, core))
    for j in range(chunks):
        send(mine, own_send.at[2, j], j, partner, center)

    def unpack(at):
        square = jnp.concatenate([buf[at, :rows, :], buf[at, rows : 2 * rows, :]], axis=1)
        diagonal = jnp.concatenate(
            [buf[at, 8 * rows : 8 * rows + 1, :], buf[at, 8 * rows + 1 : 8 * rows + 2, :]], axis=1
        )
        zero = jnp.zeros_like(square)
        tri[at, 0] = jnp.where(c >= r, square, zero)
        tri[at, 1] = jnp.where(c < r, square, jnp.where(c == r, diagonal, zero))

    def take_other(at):
        other = at + 1 - 2 * core
        for j in range(chunks):
            arrived(other, j)
        unpack(other)

    for j in range(chunks):
        arrived(b_in, j)
        hop(0, b_mate, j)
        pair(0, b_in, j)
        arrived(a_in, j)
        send(buf.at[a_in], side_send.at[0, j], j, device(b_mate), slot(a_mate - b_mate, core))
        pair(1, a_in, j)
    for j in range(chunks):
        hop(1, a_mate, j)
    for j in range(chunks):
        arrived(b_far, j)
        send(
            buf.at[b_far], side_send.at[1, j], j, device(a_mate),
            slot(cross(b_mate, place) + place - a_mate, core),
        )
        pair(2, b_far, j)
    for at in (center, a_in, b_in, b_far):
        unpack(at)
    for at in (center, a_in, b_in):
        take_other(at)
    for j in range(chunks):
        arrived(d_in, j)
        pair(3, d_in, j)
        arrived(a_far, j)
        pair(4, a_far, j)
        arrived(d_far, j)
        pair(5, d_far, j)
    for at in (d_in, a_far, d_far):
        unpack(at)
    for at in (b_far, d_in, a_far, d_far):
        take_other(at)

    scale = 1.0 / math.sqrt(B)
    for u in range(-4, 5):
        p_low[:, (u + 4) * rows : (u + 5) * rows] = (
            product(row, buf, tri, core, rows, 2, u) * scale
        ).astype(p_low.dtype)
    scale = 1.0 / math.sqrt(B) / math.sqrt(2 * B)
    for u in range(-6, 7):
        t_low[:, (u + 6) * rows : (u + 7) * rows] = (
            product(p_low, buf, tri, core, rows, 4, u) * scale
        ).astype(t_low.dtype)
    for copy in sent:
        copy.wait_send()


def last_kernel(rows, t_low, buf, tri, out, stage, out_sem):
    core = lax.axis_index("blk") % CORES
    writes = []
    done = 0
    for i, u in enumerate(range(-8, 9)):
        stage[:, i * rows : (i + 1) * rows] = product(t_low, buf, tri, core, rows, 6, u)
        if i in ENDS:
            cols = pl.ds(done * rows, (i + 1 - done) * rows)
            write = pltpu.make_async_copy(stage.at[:, cols], out.at[:, cols], out_sem.at[len(writes)])
            write.start()
            writes.append(write)
            done = i + 1
    for write in writes:
        write.wait()


def local(n, adjacency, weight):
    rows = adjacency.shape[0]
    slots = (2 * SPAN + 1) * CORES
    low = weight.dtype
    chunks = len(CUTS) + 1
    vmem = pl.BlockSpec(memory_space=pltpu.VMEM)
    hbm = pl.BlockSpec(memory_space=pltpu.HBM)
    t_low, buf, tri = pl.pallas_call(
        functools.partial(gather_kernel, n, rows),
        out_shape=(
            jax.ShapeDtypeStruct((rows, 13 * rows), low),
            jax.ShapeDtypeStruct((slots, 8 * rows + PAD, LANES), low),
            jax.ShapeDtypeStruct((slots, 2, rows, rows), low),
        ),
        in_specs=[hbm, hbm],
        out_specs=(vmem, vmem, vmem),
        scratch_shapes=[
            pltpu.VMEM(adjacency.shape, jnp.int32),
            pltpu.VMEM(weight.shape, low),
            pltpu.VMEM((rows, 5 * rows), low),
            pltpu.VMEM((rows, 9 * rows), low),
            pltpu.SemaphoreType.DMA((3, chunks)),
            pltpu.SemaphoreType.DMA((6, chunks)),
            pltpu.SemaphoreType.DMA((2, chunks)),
            pltpu.SemaphoreType.DMA((2, chunks)),
            pltpu.SemaphoreType.DMA((slots, chunks)),
            pltpu.SemaphoreType.DMA((2, 5)),
        ],
        compiler_params=pltpu.CompilerParams(
            collective_id=0, has_side_effects=True, vmem_limit_bytes=24 * 1024 * 1024
        ),
        name="gather",
    )(*(pltpu.with_memory_space_constraint(x, pltpu.HBM) for x in (adjacency, weight)))
    return pl.pallas_call(
        functools.partial(last_kernel, rows),
        out_shape=jax.ShapeDtypeStruct((rows, 17 * rows), jnp.float32),
        in_specs=[vmem, vmem, vmem],
        out_specs=hbm,
        scratch_shapes=[
            pltpu.VMEM((rows, 17 * rows), jnp.float32),
            pltpu.SemaphoreType.DMA((len(ENDS),)),
        ],
        compiler_params=pltpu.CompilerParams(vmem_limit_bytes=24 * 1024 * 1024),
        name="last",
    )(t_low, buf, tri)


def solution(mesh):
    in_specs = (P("blk", None), P("blk", None))
    out_specs = P("blk", None)
    n = mesh.shape["blk"]
    return jax.shard_map(
        functools.partial(local, n), mesh=mesh, in_specs=in_specs, out_specs=out_specs, check_vma=False
    )
```

time: 47.8 us -> 43.6 us (0.912)
  local copies, waits for them, and re-layouts: 2.13 us -> 0 us
  other arithmetic: 1.99 us -> 0 us
    unnamed x1 -> x0, local copies, waits for them, and re-layouts: 2.1 us -> none
    select_n x2 -> x0, other arithmetic: 1.93 us -> none  [the longest x1 1.87 us: banded(): return jnp.where(keep, weight, jnp.zeros_like(weight))]
    pallas_call x1 -> x2, Pallas kernels: 43.5 us -> 43.5 us  [the longest x1 39.9 us: local(): pl.pallas_call(functools.partial(gather_kernel, n, rows), out_shape=(jax....]
where the time goes in v1:
time: 43.6 us; the launch traced here: 43.5 us
  Pallas kernels  43.5 us (100%)
    pallas_call x1, Pallas kernels, local(): pl.pallas_call(functools.partial(gather_kernel, n, rows), out_shape=(jax....  39.9 us
    pallas_call x1, Pallas kernels, local(): pl.pallas_call(functools.partial(last_kernel, rows), out_shape=jax.ShapeD...  3.53 us

profile of v1, /device:TPU:1, one launch (start us, length us, event | category | flops | bytes accessed | tf_op | source)
XLA Modules:
  0.0 43.5 jit_solution(2148384492304235000)
XLA Ops:
  0.0 39.9 %gather.1 = (bf16[256,3328]{1,0:T(8,128)(2,1)S(1)}, bf16[14,2064,128]{2,1,0:T(8,128)(2,1)S(1)}, bf16[14,2,256,256]{3,2,1,0:T(8,128)(2,1)S(1)}) custom-call(s32[256,1280]{1,0:T(8,128)} %adjacency.1, bf16[256,1280]{1,0:T(8,128)(2,1)} %weight.1), custom_call_target="tpu_custom_call" | custom-call | tf_op jit(solution)/shard_map/gather/pallas_call | solution.py:245
  39.9 3.5 %last.1 = f32[256,4352]{1,0:T(8,128)} custom-call(bf16[256,3328]{1,0:T(8,128)(2,1)S(1)} %get-tuple-element.8.t_low, bf16[14,2064,128]{2,1,0:T(8,128)(2,1)S(1)} %get-tuple-element.9.buf, bf16[14,2,256,256]{3,2,1,0:T(8,128)(2,1)S(1)} %get-tuple-element.10.tri), custom_call_target="tpu_custom_call" | custom-call | tf_op jit(solution)/shard_map/last/pallas_call | solution.py:271

commit v2 on v1

v2 whole, which is shorter than its diff:
```python
import functools
import math

import jax
import jax.numpy as jnp
from jax import lax
from jax.experimental import pallas as pl
from jax.experimental.pallas import tpu as pltpu
from jax.sharding import PartitionSpec as P

B = 512
MESH = pl.DeviceIdType.MESH
CORES = 2
PLANE = 4
SPAN = PLANE - 1
LANES = 128
PAD = 16
LOADS = 2
CUTS = (128, 256, 512, 768, 1024, 1280, 1536, 1792)
SENDS = 6

OUTER = (
    (
        ("b", "me", 0), ("a", "me", 0), ("b", "me", 1), ("a", "me", 1), ("b", "me", 2), ("a", "me", 2),
        ("b", "me", 3), ("a", "me", 3), ("b", "me", 4), ("a", "me", 4), ("b", "me", 5), ("a", "me", 5),
        ("b", "me", 6), ("a", "me", 6), ("b", "me", 7), ("a", "me", 7), ("b", "me", 8), ("a", "me", 8),
    ),
    (
        ("b", 0), ("zb", "b", 0), ("a", 0), ("b", "a", 0), ("b", 1), ("zb", "b", 1), ("a", 1), ("b", "a", 1),
        ("b", 2), ("zb", "b", 2), ("a", 2), ("b", "a", 2), ("b", 3), ("zb", "b", 3), ("a", 3), ("b", "a", 3),
        ("b", 4), ("zb", "b", 4), ("a", 4), ("b", "a", 4), ("b", 5), ("zb", "b", 5), ("a", 5), ("b", "a", 5),
        ("b", 6), ("zb", "b", 6), ("a", 6), ("b", "a", 6), ("b", 7), ("zb", "b", 7), ("a", 7), ("b", "a", 7),
        ("b", 8), ("zb", "b", 8), ("a", 8), ("b", "a", 8), ("za", "a", 0), ("za", "a", 1), ("za", "a", 2),
        ("za", "a", 3), ("za", "a", 4), ("za", "a", 5), ("za", "a", 6),
    ),
    (
        ("za", "a", 7), ("za", "a", 8), ("fb", 0), ("a", "fb", 0), ("fb", 1), ("a", "fb", 1), ("fb", 2),
        ("a", "fb", 2), ("fb", 3), ("a", "fb", 3), ("fb", 4), ("a", "fb", 4), ("fb", 5), ("a", "fb", 5), ("fb", 6),
        ("a", "fb", 6), ("fb", 7), ("a", "fb", 7), ("fb", 8), ("a", "fb", 8), ("d", 0), ("fa", 0), ("fd", 0),
        ("d", 1), ("fa", 1), ("fd", 1), ("d", 2), ("fa", 2), ("fd", 2), ("d", 3), ("fa", 3), ("fd", 3), ("d", 4),
        ("fa", 4), ("fd", 4), ("d", 5), ("fa", 5), ("fd", 5), ("d", 6), ("fa", 6), ("fd", 6), ("d", 7), ("fa", 7),
        ("fd", 7), ("d", 8), ("fa", 8), ("fd", 8),
    ),
    (
    ),
    (
    ),
    (
    ),
    (
    ),
    (
    ),
    (
    ),
    (
    ),
)
INNER = (
    (
        ("b", "me", 0), ("a", "me", 0), ("b", "me", 1), ("a", "me", 1), ("b", "me", 2), ("a", "me", 2),
        ("b", "me", 3), ("a", "me", 3), ("b", "me", 4), ("a", "me", 4), ("b", "me", 5), ("a", "me", 5),
        ("b", "me", 6), ("a", "me", 6), ("b", "me", 7), ("a", "me", 7), ("b", "me", 8), ("a", "me", 8),
    ),
    (
        ("b", 0), ("zb", "b", 0), ("a", 0), ("b", "a", 0), ("b", 1), ("zb", "b", 1), ("a", 1), ("b", "a", 1),
        ("b", 2), ("zb", "b", 2), ("a", 2), ("b", "a", 2), ("b", 3), ("zb", "b", 3), ("a", 3), ("b", "a", 3),
        ("b", 4), ("zb", "b", 4), ("a", 4), ("b", "a", 4), ("b", 5), ("zb", "b", 5), ("a", 5), ("b", "a", 5),
        ("b", 6), ("zb", "b", 6), ("a", 6), ("b", "a", 6), ("b", 7), ("zb", "b", 7), ("a", 7), ("b", "a", 7),
        ("b", 8), ("zb", "b", 8), ("a", 8), ("b", "a", 8), ("za", "a", 0), ("za", "a", 1), ("za", "a", 2),
        ("za", "a", 3), ("za", "a", 4), ("za", "a", 5), ("za", "a", 6),
    ),
    (
        ("za", "a", 7), ("za", "a", 8), ("fb", 0), ("a", "fb", 0), ("fb", 1), ("a", "fb", 1), ("fb", 2),
        ("a", "fb", 2), ("fb", 3), ("a", "fb", 3), ("fb", 4), ("a", "fb", 4), ("fb", 5), ("a", "fb", 5), ("fb", 6),
        ("a", "fb", 6), ("fb", 7), ("a", "fb", 7), ("fb", 8), ("a", "fb", 8), ("d", 0), ("fa", 0), ("fd", 0),
        ("d", 1), ("fa", 1), ("fd", 1), ("d", 2), ("fa", 2), ("fd", 2), ("d", 3), ("fa", 3), ("fd", 3), ("d", 4),
        ("fa", 4), ("fd", 4), ("d", 5), ("fa", 5), ("fd", 5), ("d", 6), ("fa", 6), ("fd", 6), ("d", 7), ("fa", 7),
        ("fd", 7), ("d", 8), ("fa", 8),
    ),
    (
    ),
    (
    ),
    (
    ),
    (
    ),
    (
    ),
    (
    ),
    (
        ("fd", 8),
    ),
)
SPANS = ((-8, -5), (-5, -2), (3, 6), (6, 9))


def block_of(buf, tri, at, k, rows):
    if k in (0, 4):
        return tri[at, k // 4]
    low = 2 * k * rows
    return jnp.concatenate([buf[at, low : low + rows, :], buf[at, low + rows : low + 2 * rows, :]], axis=1)


def ends_of(buf, at, rows):
    r = lax.broadcasted_iota(jnp.int32, (rows, rows), 0)
    c = lax.broadcasted_iota(jnp.int32, (rows, rows), 1)
    square = jnp.concatenate([buf[at, :rows, :], buf[at, rows : 2 * rows, :]], axis=1)
    diagonal = jnp.concatenate(
        [buf[at, 8 * rows : 8 * rows + 1, :], buf[at, 8 * rows + 1 : 8 * rows + 2, :]], axis=1
    )
    zero = jnp.zeros_like(square)
    return jnp.where(c >= r, square, zero), jnp.where(c < r, square, jnp.where(c == r, diagonal, zero))


def product(left, buf, tri, core, rows, reach, u, only):
    terms = [m for m in only if abs(u - m) <= 2]
    right = jnp.concatenate([block_of(buf, tri, m + 2 * SPAN + core, u - m + 2, rows) for m in terms], axis=0)
    low, high = terms[0] + reach, terms[-1] + reach
    return jnp.dot(left[:, low * rows : (high + 1) * rows], right, preferred_element_type=jnp.float32)


def gather_kernel(
    n, rows, adjacency, weight, t_low, partial, buf, adj, wgt, row, p_low, tri, via,
    send_sem, pair_send, recv, pair_recv, via_recv, in_sem,
):
    me = lax.axis_index("blk")
    core = me % CORES
    place = (me // CORES) % PLANE
    group = me // (CORES * PLANE)
    groups = n // (CORES * PLANE)
    partner = me + 1 - 2 * core
    up = ((group + 1) % groups * PLANE + place) * CORES + core
    down = ((group + groups - 1) % groups * PLANE + place) * CORES + core
    x_mate = place + 1 - 2 * (place % 2)
    y_mate = (place + 2) % PLANE
    inner = (place + 1) // 2 % 2
    a_mate = (1 - inner) * x_mate + inner * y_mate
    b_mate = inner * x_mate + (1 - inner) * y_mate
    d_mate = SPAN - place

    def device(q):
        return (group * PLANE + q) * CORES + core

    def is_above(q, p):
        return (q - p + PLANE) // PLANE

    def cross(q, p):
        return q - p + PLANE - 2 * PLANE * is_above(q, p)

    def either(outer_one, inner_one):
        return outer_one + inner * (inner_one - outer_one)

    def beyond(q):
        above = is_above(q, place)
        return above * up + (1 - above) * down

    total = buf.shape[1]
    bounds = [(s, e - s) for s, e in zip((0,) + CUTS, CUTS + (total,))]
    chunks = range(len(bounds))

    mates = {"a": a_mate, "b": b_mate, "d": d_mate}
    chip = {"me": 0 * place}
    for name, q in mates.items():
        chip[name] = q - place
        chip["f" + name] = cross(q, place)
    device_of = {"a": device(a_mate), "b": device(b_mate)}
    for name, q in mates.items():
        device_of["z" + name] = beyond(q)
    device_of["k0"] = up + down - device_of["zb"]
    device_of["k1"] = up + down - device_of["za"]
    place_of = {"a": place - a_mate, "b": place - b_mate}
    own_via = {m: cross(place, mates[m]) for m in ("a", "b")}

    def slot(chip_offset):
        return (chip_offset + SPAN) * CORES + core

    barrier = pltpu.get_barrier_semaphore()
    greeted = [partner, up, down, device_of["a"], device_of["b"]]
    for other in greeted:
        pl.semaphore_signal(barrier, inc=1, device_id=(other,), device_id_type=MESH)

    step = rows // LOADS
    loads = []
    for i in range(LOADS):
        part = pl.ds(i * step, step)
        loads.append((
            pltpu.make_async_copy(adjacency.at[part], adj.at[part], in_sem.at[0, i]),
            pltpu.make_async_copy(weight.at[part], wgt.at[part], in_sem.at[1, i]),
        ))
    for pair_of in loads:
        for load in pair_of:
            load.start()

    center = slot(0)
    diagonal = jnp.zeros((1, rows), jnp.float32)
    for i, pair_of in enumerate(loads):
        for load in pair_of:
            load.wait()
        part = slice(i * step, (i + 1) * step)
        r = lax.broadcasted_iota(jnp.int32, (step, rows), 0) + i * step
        c = lax.broadcasted_iota(jnp.int32, (step, rows), 1)
        kept = []
        for k in range(5):
            cols = slice(k * rows, (k + 1) * rows)
            keep = adj[part, cols] == 1
            if k == 0:
                keep &= c >= r
            elif k == 2:
                keep |= c == r
            elif k == 4:
                keep &= c <= r
            kept.append(jnp.where(keep, wgt[part, cols].astype(jnp.float32), 0.0))
            row[part, cols] = kept[k].astype(row.dtype)
        packed = [jnp.where(c >= r, kept[0], kept[4])] + kept[1:4]
        for k in range(4):
            low = packed[k].astype(row.dtype)
            for h in range(2):
                start = (2 * k + h) * rows + i * step
                buf[center, start : start + step, :] = low[:, h * LANES : (h + 1) * LANES]
        diagonal += jnp.sum(jnp.where(c == r, kept[4], 0.0), axis=0, keepdims=True)
    tail = jnp.concatenate(
        [diagonal[:, :LANES], diagonal[:, LANES:], jnp.zeros((PAD - 2, LANES), jnp.float32)], axis=0
    )
    buf[center, 8 * rows :, :] = tail.astype(row.dtype)
    pl.semaphore_wait(barrier, len(greeted))

    def chunk(at, j):
        return buf.at[at, pl.ds(bounds[j][0], bounds[j][1])]

    def arrive(chip_offset, j):
        return recv.at[chip_offset + SPAN, j]

    def remote(source, target, sem, arrival, to):
        return pltpu.make_async_remote_copy(
            src_ref=source, dst_ref=target, send_sem=sem, recv_sem=arrival, device_id=(to,), device_id_type=MESH
        )

    def pair(chip_offset, j):
        at = slot(chip_offset)
        remote(chunk(at, j), chunk(at, j), pair_send, pair_recv.at[chip_offset + SPAN], partner).start()

    classes = []
    sent = ({}, {})

    def send(kind, link, name, j):
        key = (link, name)
        if key not in classes:
            classes.append(key)
        sem = send_sem.at[classes.index(key)]
        sent[kind][key] = sent[kind].get(key, 0) + bounds[j][1]
        to = device_of[link]
        if link[0] == "k":
            i = int(link[1])
            remote(chunk(center, j), via.at[i], sem, via_recv.at[i], to).start()
        elif name[0] == "v":
            there = own_via[link]
            remote(via.at[int(name[1])], chunk(slot(there), j), sem, arrive(there, j), to).start()
        else:
            there = chip["f" + name] if link[0] == "z" else chip[name] + place_of[link]
            remote(chunk(slot(chip[name]), j), chunk(slot(there), j), sem, arrive(there, j), to).start()

    def take(name, j):
        if name[0] == "v":
            i = int(name[1])
            pltpu.make_async_copy(chunk(center, j), via.at[i], via_recv.at[i]).wait()
            return
        at = slot(chip[name])
        pltpu.make_async_copy(chunk(center, j), chunk(at, j), arrive(chip[name], j)).wait()
        pair(chip[name], j)

    def perform(index):
        for kind, steps in enumerate((OUTER, INNER)):
            def body(kind=kind, steps=steps):
                for op in steps[index]:
                    if len(op) == 2:
                        take(*op)
                    else:
                        send(kind, *op)

            pl.when(inner == kind)(body)

    def take_other(chip_offset):
        at = slot(chip_offset) + 1 - 2 * core
        pltpu.make_async_copy(buf.at[center], buf.at[at], pair_recv.at[chip_offset + SPAN]).wait()

    def unpack(at):
        tri[at, 0], tri[at, 1] = ends_of(buf, at, rows)

    near = ("me", "a", "b")
    near_z, near_plane = either(chip["fb"], chip["fa"]), either(chip["fd"], chip["d"])
    far_z, far_plane = either(chip["fa"], chip["fb"]), either(chip["d"], chip["fd"])

    perform(0)
    for j in chunks:
        pair(chip["me"], j)
    unpack(center)
    perform(1)
    for name in near:
        if name != "me":
            unpack(slot(chip[name]))
        take_other(chip[name])
        unpack(slot(chip[name]) + 1 - 2 * core)
    perform(2)
    for offset in (near_z, near_plane):
        unpack(slot(offset))
        take_other(offset)
        unpack(slot(offset) + 1 - 2 * core)

    scale = 1.0 / math.sqrt(B)
    for u in range(-4, 5):
        p_low[:, (u + 4) * rows : (u + 5) * rows] = (
            product(row, buf, tri, core, rows, 2, u, range(-2, 3)) * scale
        ).astype(p_low.dtype)
    perform(3)
    scale = 1.0 / math.sqrt(B) / math.sqrt(2 * B)
    for u in range(-6, 7):
        t_low[:, (u + 6) * rows : (u + 7) * rows] = (
            product(p_low, buf, tri, core, rows, 4, u, range(-4, 5)) * scale
        ).astype(t_low.dtype)
        if u in (-2, 2, 6):
            perform({-2: 4, 2: 5, 6: 6}[u])
    for u in range(-6, 7):
        partial[:, (u + 6) * rows : (u + 7) * rows] = product(t_low, buf, tri, core, rows, 6, u, range(-4, 5))
        if u in (-2, 2, 6):
            perform({-2: 7, 2: 8, 6: 9}[u])
    for offset in (far_z, far_plane):
        take_other(offset)

    def sent_out(size, sem):
        part = buf.at[center, pl.ds(0, size)]
        remote(part, part, sem, via_recv.at[0], partner).wait_send()

    blocks = buf.at[pl.ds(0, 2 * SPAN + 1)]
    remote(blocks, blocks, pair_send, via_recv.at[0], partner).wait_send()
    for kind in range(2):
        def finish(kind=kind):
            for key, size in sent[kind].items():
                sent_out(size, send_sem.at[classes.index(key)])

        pl.when(inner == kind)(finish)


def last_kernel(rows, t_low, partial, buf, out, tri, stage, out_sem):
    core = lax.axis_index("blk") % CORES
    far = (-6, -5, 5, 6)
    middle = pl.ds(6 * rows, 5 * rows)
    writes = [pltpu.make_async_copy(partial.at[:, pl.ds(4 * rows, 5 * rows)], out.at[:, middle], out_sem.at[0])]
    writes[0].start()
    for i, m in enumerate(far):
        tri[i, 0], tri[i, 1] = ends_of(buf, m + 2 * SPAN + core, rows)
    for low, high in SPANS:
        for u in range(low, high):
            terms = [(i, m) for i, m in enumerate(far) if abs(u - m) <= 2]
            right = []
            for i, m in terms:
                k = u - m + 2
                at = m + 2 * SPAN + core
                right.append(tri[i, k // 4] if k in (0, 4) else block_of(buf, None, at, k, rows))
            first, last = terms[0][1] + 6, terms[-1][1] + 6
            value = jnp.dot(
                t_low[:, first * rows : (last + 1) * rows], jnp.concatenate(right, axis=0),
                preferred_element_type=jnp.float32,
            )
            if abs(u) <= 6:
                value += partial[:, (u + 6) * rows : (u + 7) * rows]
            stage[:, (u + 8) * rows : (u + 9) * rows] = value
        cols = pl.ds((low + 8) * rows, (high - low) * rows)
        write = pltpu.make_async_copy(stage.at[:, cols], out.at[:, cols], out_sem.at[len(writes)])
        write.start()
        writes.append(write)
    for write in writes:
        write.wait()


def local(n, adjacency, weight):
    rows = adjacency.shape[0]
    slots = (2 * SPAN + 1) * CORES
    low = weight.dtype
    chunks = len(CUTS) + 1
    vmem = pl.BlockSpec(memory_space=pltpu.VMEM)
    hbm = pl.BlockSpec(memory_space=pltpu.HBM)
    t_low, partial, buf = pl.pallas_call(
        functools.partial(gather_kernel, n, rows),
        out_shape=(
            jax.ShapeDtypeStruct((rows, 13 * rows), low),
            jax.ShapeDtypeStruct((rows, 13 * rows), jnp.float32),
            jax.ShapeDtypeStruct((slots, 8 * rows + PAD, LANES), low),
        ),
        in_specs=[hbm, hbm],
        out_specs=(vmem, vmem, vmem),
        scratch_shapes=[
            pltpu.VMEM(adjacency.shape, jnp.int32),
            pltpu.VMEM(weight.shape, low),
            pltpu.VMEM((rows, 5 * rows), low),
            pltpu.VMEM((rows, 9 * rows), low),
            pltpu.VMEM((slots, 2, rows, rows), low),
            pltpu.VMEM((2, CUTS[0], LANES), low),
            pltpu.SemaphoreType.DMA((SENDS,)),
            pltpu.SemaphoreType.DMA,
            pltpu.SemaphoreType.DMA((2 * SPAN + 1, chunks)),
            pltpu.SemaphoreType.DMA((2 * SPAN + 1,)),
            pltpu.SemaphoreType.DMA((2,)),
            pltpu.SemaphoreType.DMA((2, LOADS)),
        ],
        compiler_params=pltpu.CompilerParams(
            collective_id=0, has_side_effects=True, vmem_limit_bytes=24 * 1024 * 1024
        ),
        name="gather",
    )(*(pltpu.with_memory_space_constraint(x, pltpu.HBM) for x in (adjacency, weight)))
    return pl.pallas_call(
        functools.partial(last_kernel, rows),
        out_shape=jax.ShapeDtypeStruct((rows, 17 * rows), jnp.float32),
        in_specs=[vmem, vmem, vmem],
        out_specs=hbm,
        scratch_shapes=[
            pltpu.VMEM((4, 2, rows, rows), low),
            pltpu.VMEM((rows, 17 * rows), jnp.float32),
            pltpu.SemaphoreType.DMA((len(SPANS) + 1,)),
        ],
        compiler_params=pltpu.CompilerParams(vmem_limit_bytes=24 * 1024 * 1024),
        name="last",
    )(t_low, partial, buf)


def solution(mesh):
    in_specs = (P("blk", None), P("blk", None))
    out_specs = P("blk", None)
    n = mesh.shape["blk"]
    return jax.shard_map(
        functools.partial(local, n), mesh=mesh, in_specs=in_specs, out_specs=out_specs, check_vma=False
    )
```

time: 43.6 us -> 42.1 us (0.966)
  Pallas kernels: 43.5 us -> 41.9 us
    pallas_call x1, Pallas kernels: 3.53 us -> 2.14 us  [local(): pl.pallas_call(functools.partial(last_kernel, rows), out_shape=jax.ShapeD...]
where the time goes in v2:
time: 42.1 us; the launch traced here: 41.9 us
  Pallas kernels  41.9 us (100%)
    pallas_call x1, Pallas kernels, local(): pl.pallas_call(functools.partial(gather_kernel, n, rows), out_shape=(jax....  39.8 us
    pallas_call x1, Pallas kernels, local(): pl.pallas_call(functools.partial(last_kernel, rows), out_shape=jax.ShapeD...  2.14 us

profile of v2, /device:TPU:1, one launch (start us, length us, event | category | flops | bytes accessed | tf_op | source)
XLA Modules:
  0.0 41.9 jit_solution(5992776620157348785)
XLA Ops:
  0.0 39.8 %gather.1 = (bf16[256,3328]{1,0:T(8,128)(2,1)S(1)}, f32[256,3328]{1,0:T(8,128)S(1)}, bf16[14,2064,128]{2,1,0:T(8,128)(2,1)S(1)}) custom-call(s32[256,1280]{1,0:T(8,128)} %adjacency.1, bf16[256,1280]{1,0:T(8,128)(2,1)} %weight.1), custom_call_target="tpu_custom_call" | custom-call | tf_op jit(solution)/shard_map/gather/pallas_call | solution.py:385
  39.8 2.1 %last.1 = f32[256,4352]{1,0:T(8,128)} custom-call(bf16[256,3328]{1,0:T(8,128)(2,1)S(1)} %get-tuple-element.8.t_low, f32[256,3328]{1,0:T(8,128)S(1)} %get-tuple-element.9.partial, bf16[14,2064,128]{2,1,0:T(8,128)(2,1)S(1)} %get-tuple-element.10.buf), custom_call_target="tpu_custom_call" | custom-call | tf_op jit(solution)/shard_map/last/pallas_call | solution.py:413

commit v3 on v2

v3 whole, which is shorter than its diff:
```python
import functools
import math

import jax
import jax.numpy as jnp
from jax import lax
from jax.experimental import pallas as pl
from jax.experimental.pallas import tpu as pltpu
from jax.sharding import PartitionSpec as P

B = 512
MESH = pl.DeviceIdType.MESH
CORES = 2
PLANE = 4
SPAN = PLANE - 1
LANES = 128
PAD = 16
LOADS = 2
CUTS = (256, 512, 768, 1024, 1280, 1536, 1792)
LAG = 3
SENT_BLOCKS = 2 + 2 + 2 + (2 * SPAN + 1)
FORWARDS_T = {-2: (0, 1), 2: (2, 3), 6: (4,)}
FORWARDS_OUT = {-2: (5,), 2: (6,), 6: (7,)}
SPANS = ((-8, -5), (-5, -2), (3, 6), (6, 9))


def block_of(buf, tri, at, k, rows):
    if k in (0, 4):
        return tri[at, k // 4]
    low = 2 * k * rows
    return jnp.concatenate([buf[at, low : low + rows, :], buf[at, low + rows : low + 2 * rows, :]], axis=1)


def ends_of(buf, at, rows):
    r = lax.broadcasted_iota(jnp.int32, (rows, rows), 0)
    c = lax.broadcasted_iota(jnp.int32, (rows, rows), 1)
    square = jnp.concatenate([buf[at, :rows, :], buf[at, rows : 2 * rows, :]], axis=1)
    diagonal = jnp.concatenate(
        [buf[at, 8 * rows : 8 * rows + 1, :], buf[at, 8 * rows + 1 : 8 * rows + 2, :]], axis=1
    )
    zero = jnp.zeros_like(square)
    return jnp.where(c >= r, square, zero), jnp.where(c < r, square, jnp.where(c == r, diagonal, zero))


def product(left, buf, tri, core, rows, reach, u, only):
    terms = [m for m in only if abs(u - m) <= 2]
    right = jnp.concatenate([block_of(buf, tri, m + 2 * SPAN + core, u - m + 2, rows) for m in terms], axis=0)
    low, high = terms[0] + reach, terms[-1] + reach
    return jnp.dot(left[:, low * rows : (high + 1) * rows], right, preferred_element_type=jnp.float32)


def gather_kernel(
    n, rows, adjacency, weight, t_low, partial, buf, adj, wgt, row, p_low, tri,
    send_sem, recv, pair_recv, in_sem,
):
    me = lax.axis_index("blk")
    core = me % CORES
    place = (me // CORES) % PLANE
    group = me // (CORES * PLANE)
    groups = n // (CORES * PLANE)
    partner = me + 1 - 2 * core
    up = ((group + 1) % groups * PLANE + place) * CORES + core
    down = ((group + groups - 1) % groups * PLANE + place) * CORES + core
    x_mate = place + 1 - 2 * (place % 2)
    y_mate = (place + 2) % PLANE
    d_mate = SPAN - place
    inner = (place + 1) // 2 % 2

    def device(q):
        return (group * PLANE + q) * CORES + core

    def is_above(q, p):
        return (q - p + PLANE) // PLANE

    def cross(q, p):
        return q - p + PLANE - 2 * PLANE * is_above(q, p)

    def either(outer_one, inner_one):
        return outer_one + inner * (inner_one - outer_one)

    def slot(offset):
        return (offset + SPAN) * CORES + core

    total = buf.shape[1]
    bounds = [(s, e - s) for s, e in zip((0,) + CUTS, CUTS + (total,))]
    chunks = range(len(bounds))
    x_dev, y_dev = device(x_mate), device(y_mate)

    barrier = pltpu.get_barrier_semaphore()
    greeted = [partner, up, down, x_dev, y_dev]
    for other in greeted:
        pl.semaphore_signal(barrier, inc=1, device_id=(other,), device_id_type=MESH)

    step = rows // LOADS
    loads = []
    for i in range(LOADS):
        part = pl.ds(i * step, step)
        loads.append((
            pltpu.make_async_copy(adjacency.at[part], adj.at[part], in_sem.at[0, i]),
            pltpu.make_async_copy(weight.at[part], wgt.at[part], in_sem.at[1, i]),
        ))
    for pair_of in loads:
        for load in pair_of:
            load.start()

    center = slot(0)
    diagonal = jnp.zeros((1, rows), jnp.float32)
    for i, pair_of in enumerate(loads):
        for load in pair_of:
            load.wait()
        part = slice(i * step, (i + 1) * step)
        r = lax.broadcasted_iota(jnp.int32, (step, rows), 0) + i * step
        c = lax.broadcasted_iota(jnp.int32, (step, rows), 1)
        kept = []
        for k in range(5):
            cols = slice(k * rows, (k + 1) * rows)
            keep = adj[part, cols] == 1
            if k == 0:
                keep &= c >= r
            elif k == 2:
                keep |= c == r
            elif k == 4:
                keep &= c <= r
            kept.append(jnp.where(keep, wgt[part, cols].astype(jnp.float32), 0.0))
            row[part, cols] = kept[k].astype(row.dtype)
        packed = [jnp.where(c >= r, kept[0], kept[4])] + kept[1:4]
        for k in range(4):
            low = packed[k].astype(row.dtype)
            for h in range(2):
                start = (2 * k + h) * rows + i * step
                buf[center, start : start + step, :] = low[:, h * LANES : (h + 1) * LANES]
        diagonal += jnp.sum(jnp.where(c == r, kept[4], 0.0), axis=0, keepdims=True)
    tail = jnp.concatenate(
        [diagonal[:, :LANES], diagonal[:, LANES:], jnp.zeros((PAD - 2, LANES), jnp.float32)], axis=0
    )
    buf[center, 8 * rows :, :] = tail.astype(row.dtype)
    pl.semaphore_wait(barrier, len(greeted))

    def chunk(offset, j):
        return buf.at[slot(offset), pl.ds(bounds[j][0], bounds[j][1])]

    def arrival(offset, j):
        return recv.at[offset + SPAN - (offset + SPAN) // (SPAN + 1), j]

    def remote(source, target, sem, to):
        return pltpu.make_async_remote_copy(
            src_ref=source, dst_ref=target, send_sem=send_sem, recv_sem=sem, device_id=(to,), device_id_type=MESH
        )

    def send(offset, j, to, there):
        remote(chunk(offset, j), chunk(there, j), arrival(there, j), to).start()

    def pair(offset, j):
        remote(chunk(offset, j), chunk(offset, j), pair_recv.at[offset + SPAN], partner).start()

    def take(offset, j):
        pltpu.make_async_copy(chunk(0, j), chunk(offset, j), arrival(offset, j)).wait()

    def take_pair(offset, j):
        take(offset, j)
        pair(offset, j)

    def hop(q, j):
        above = is_above(q, place)
        send(q - place, j, above * up + (1 - above) * down, cross(q, place))

    def other(offset):
        return slot(offset) + 1 - 2 * core

    def unpack(at):
        tri[at, 0], tri[at, 1] = ends_of(buf, at, rows)

    def unpack_own(offset):
        unpack(slot(offset))

    def unpack_other(offset):
        at = other(offset)
        pltpu.make_async_copy(buf.at[center], buf.at[at], pair_recv.at[offset + SPAN]).wait()
        unpack(at)

    x, y, d = (q - place for q in (x_mate, y_mate, d_mate))
    x_far, y_far, d_far = (cross(q, place) for q in (x_mate, y_mate, d_mate))
    near, far = either(d_far, d), either(d, d_far)

    for j in chunks:
        send(0, j, y_dev, place - y_mate)
        send(0, j, x_dev, place - x_mate)
    for j in chunks:
        pair(0, j)
    unpack_own(0)
    def relay_far(j):
        take(y_far, j)
        send(y_far, j, x_dev, y_far + place - x_mate)
        pair(y_far, j)

    for j in chunks:
        take(y, j)
        hop(y_mate, j)
        pair(y, j)
        take(x, j)
        send(x, j, y_dev, x_mate - y_mate)
        pair(x, j)
        if j >= LAG:
            relay_far(j - LAG)
    for j in chunks:
        hop(x_mate, j)
    for j in chunks[-LAG:]:
        relay_far(j)
    unpack_other(0)
    for offset in (x, y, y_far):
        unpack_own(offset)
        unpack_other(offset)
    for j in chunks:
        take_pair(near, j)
    for j in chunks[:4]:
        take_pair(far, j)
    unpack_own(near)
    unpack_other(near)

    scale = 1.0 / math.sqrt(B)
    for u in range(-4, 5):
        p_low[:, (u + 4) * rows : (u + 5) * rows] = (
            product(row, buf, tri, core, rows, 2, u, range(-2, 3)) * scale
        ).astype(p_low.dtype)
    for j in chunks[4:]:
        take_pair(far, j)
    scale = 1.0 / math.sqrt(B) / math.sqrt(2 * B)
    for u in range(-6, 7):
        t_low[:, (u + 6) * rows : (u + 7) * rows] = (
            product(p_low, buf, tri, core, rows, 4, u, range(-4, 5)) * scale
        ).astype(t_low.dtype)
        for j in FORWARDS_T.get(u, ()):
            take_pair(x_far, j)
    for u in range(-6, 7):
        partial[:, (u + 6) * rows : (u + 7) * rows] = product(t_low, buf, tri, core, rows, 6, u, range(-4, 5))
        for j in FORWARDS_OUT.get(u, ()):
            take_pair(x_far, j)
    for offset in (far, x_far):
        pltpu.make_async_copy(buf.at[center], buf.at[other(offset)], pair_recv.at[offset + SPAN]).wait()
    blocks = buf.at[pl.ds(0, SENT_BLOCKS)]
    remote(blocks, blocks, pair_recv.at[0], partner).wait_send()


def last_kernel(rows, t_low, partial, buf, out, tri, stage, out_sem):
    core = lax.axis_index("blk") % CORES
    far = (-6, -5, 5, 6)
    middle = pl.ds(6 * rows, 5 * rows)
    writes = [pltpu.make_async_copy(partial.at[:, pl.ds(4 * rows, 5 * rows)], out.at[:, middle], out_sem.at[0])]
    writes[0].start()
    for i, m in enumerate(far):
        tri[i, 0], tri[i, 1] = ends_of(buf, m + 2 * SPAN + core, rows)
    for low, high in SPANS:
        for u in range(low, high):
            terms = [(i, m) for i, m in enumerate(far) if abs(u - m) <= 2]
            right = []
            for i, m in terms:
                k = u - m + 2
                at = m + 2 * SPAN + core
                right.append(tri[i, k // 4] if k in (0, 4) else block_of(buf, None, at, k, rows))
            first, last = terms[0][1] + 6, terms[-1][1] + 6
            value = jnp.dot(
                t_low[:, first * rows : (last + 1) * rows], jnp.concatenate(right, axis=0),
                preferred_element_type=jnp.float32,
            )
            if abs(u) <= 6:
                value += partial[:, (u + 6) * rows : (u + 7) * rows]
            stage[:, (u + 8) * rows : (u + 9) * rows] = value
        cols = pl.ds((low + 8) * rows, (high - low) * rows)
        write = pltpu.make_async_copy(stage.at[:, cols], out.at[:, cols], out_sem.at[len(writes)])
        write.start()
        writes.append(write)
    for write in writes:
        write.wait()


def local(n, adjacency, weight):
    rows = adjacency.shape[0]
    slots = (2 * SPAN + 1) * CORES
    low = weight.dtype
    chunks = len(CUTS) + 1
    vmem = pl.BlockSpec(memory_space=pltpu.VMEM)
    hbm = pl.BlockSpec(memory_space=pltpu.HBM)
    t_low, partial, buf = pl.pallas_call(
        functools.partial(gather_kernel, n, rows),
        out_shape=(
            jax.ShapeDtypeStruct((rows, 13 * rows), low),
            jax.ShapeDtypeStruct((rows, 13 * rows), jnp.float32),
            jax.ShapeDtypeStruct((slots, 8 * rows + PAD, LANES), low),
        ),
        in_specs=[hbm, hbm],
        out_specs=(vmem, vmem, vmem),
        scratch_shapes=[
            pltpu.VMEM(adjacency.shape, jnp.int32),
            pltpu.VMEM(weight.shape, low),
            pltpu.VMEM((rows, 5 * rows), low),
            pltpu.VMEM((rows, 9 * rows), low),
            pltpu.VMEM((slots, 2, rows, rows), low),
            pltpu.SemaphoreType.DMA,
            pltpu.SemaphoreType.DMA((2 * SPAN, chunks)),
            pltpu.SemaphoreType.DMA((2 * SPAN + 1,)),
            pltpu.SemaphoreType.DMA((2, LOADS)),
        ],
        compiler_params=pltpu.CompilerParams(
            collective_id=0, has_side_effects=True, vmem_limit_bytes=24 * 1024 * 1024
        ),
        name="gather",
    )(*(pltpu.with_memory_space_constraint(x, pltpu.HBM) for x in (adjacency, weight)))
    return pl.pallas_call(
        functools.partial(last_kernel, rows),
        out_shape=jax.ShapeDtypeStruct((rows, 17 * rows), jnp.float32),
        in_specs=[vmem, vmem, vmem],
        out_specs=hbm,
        scratch_shapes=[
            pltpu.VMEM((4, 2, rows, rows), low),
            pltpu.VMEM((rows, 17 * rows), jnp.float32),
            pltpu.SemaphoreType.DMA((len(SPANS) + 1,)),
        ],
        compiler_params=pltpu.CompilerParams(vmem_limit_bytes=24 * 1024 * 1024),
        name="last",
    )(t_low, partial, buf)


def solution(mesh):
    in_specs = (P("blk", None), P("blk", None))
    out_specs = P("blk", None)
    n = mesh.shape["blk"]
    return jax.shard_map(
        functools.partial(local, n), mesh=mesh, in_specs=in_specs, out_specs=out_specs, check_vma=False
    )
```

time: 42.1 us -> 40.1 us (0.952)
  Pallas kernels: 41.9 us -> 39.6 us
    pallas_call x1, Pallas kernels: 39.8 us -> 37.4 us  [local(): pl.pallas_call(functools.partial(gather_kernel, n, rows), out_shape=(jax....]
where the time goes in v3:
time: 40.1 us; the launch traced here: 39.6 us
  Pallas kernels  39.6 us (99%)
    pallas_call x1, Pallas kernels, local(): pl.pallas_call(functools.partial(gather_kernel, n, rows), out_shape=(jax....  37.4 us
    pallas_call x1, Pallas kernels, local(): pl.pallas_call(functools.partial(last_kernel, rows), out_shape=jax.ShapeD...  2.14 us

profile of v3, /device:TPU:1, one launch (start us, length us, event | category | flops | bytes accessed | tf_op | source)
XLA Modules:
  0.0 39.6 jit_solution(15277199963747938235)
XLA Ops:
  0.0 37.4 %gather.1 = (bf16[256,3328]{1,0:T(8,128)(2,1)S(1)}, f32[256,3328]{1,0:T(8,128)S(1)}, bf16[14,2064,128]{2,1,0:T(8,128)(2,1)S(1)}) custom-call(s32[256,1280]{1,0:T(8,128)} %adjacency.1, bf16[256,1280]{1,0:T(8,128)(2,1)} %weight.1), custom_call_target="tpu_custom_call" | custom-call | tf_op jit(solution)/shard_map/gather/pallas_call | solution.py:283
  37.4 2.1 %last.1 = f32[256,4352]{1,0:T(8,128)} custom-call(bf16[256,3328]{1,0:T(8,128)(2,1)S(1)} %get-tuple-element.8.t_low, f32[256,3328]{1,0:T(8,128)S(1)} %get-tuple-element.9.partial, bf16[14,2064,128]{2,1,0:T(8,128)(2,1)S(1)} %get-tuple-element.10.buf), custom_call_target="tpu_custom_call" | custom-call | tf_op jit(solution)/shard_map/last/pallas_call | solution.py:308

commit v4 on v3

--- a/solution.py
+++ b/solution.py
@@ -19,8 +19,12 @@
 CUTS = (256, 512, 768, 1024, 1280, 1536, 1792)
 LAG = 3
 SENT_BLOCKS = 2 + 2 + 2 + (2 * SPAN + 1)
-FORWARDS_T = {-2: (0, 1), 2: (2, 3), 6: (4,)}
-FORWARDS_OUT = {-2: (5,), 2: (6,), 6: (7,)}
+FORWARDS = (
+    ((0, 0), (0, 1), (0, 2), (0, 3), (1, 1), (1, 2), (1, 3)),
+    ((0, 4), (0, 5), (0, 6), (0, 7), (1, 4)),
+)
+FORWARDS_T = {-3: ((1, 5),), 0: ((1, 6),), 3: ((1, 0), (1, 7))}
+FORWARDS_OUT = {}
 SPANS = ((-8, -5), (-5, -2), (3, 6), (6, 9))
 
 
@@ -50,8 +54,8 @@
 
 
 def gather_kernel(
-    n, rows, adjacency, weight, t_low, partial, buf, adj, wgt, row, p_low, tri,
-    send_sem, recv, pair_recv, in_sem,
+    n, rows, adjacency, weight, t_low, partial, buf, adj, wgt, row, p_low, tri, via, p_early, t_early,
+    send_sem, relay_sem, recv, pair_recv, via_recv, in_sem,
 ):
     me = lax.axis_index("blk")
     core = me % CORES
@@ -160,9 +164,12 @@
         take(offset, j)
         pair(offset, j)
 
+    def beyond(q):
+        above = is_above(q, place)
+        return above * up + (1 - above) * down
+
     def hop(q, j):
-        above = is_above(q, place)
-        send(q - place, j, above * up + (1 - above) * down, cross(q, place))
+        send(q - place, j, beyond(q), cross(q, place))
 
     def other(offset):
         return slot(offset) + 1 - 2 * core
@@ -182,6 +189,7 @@
     x_far, y_far, d_far = (cross(q, place) for q in (x_mate, y_mate, d_mate))
     near, far = either(d_far, d), either(d, d_far)
 
+    remote(chunk(0, 0), via, via_recv, up + down - beyond(x_mate)).start()
     for j in chunks:
         send(0, j, y_dev, place - y_mate)
         send(0, j, x_dev, place - x_mate)
@@ -202,43 +210,89 @@
         pair(x, j)
         if j >= LAG:
             relay_far(j - LAG)
-    for j in chunks:
+    for j in chunks[1:]:
         hop(x_mate, j)
     for j in chunks[-LAG:]:
         relay_far(j)
+    pltpu.make_async_copy(chunk(0, 0), via, via_recv).wait()
+    handed = cross(place, x_mate)
+    relay = pltpu.make_async_remote_copy(
+        src_ref=via, dst_ref=chunk(handed, 0), send_sem=relay_sem, recv_sem=arrival(handed, 0),
+        device_id=(x_dev,), device_id_type=MESH,
+    )
+    relay.start()
     unpack_other(0)
     for offset in (x, y, y_far):
         unpack_own(offset)
         unpack_other(offset)
+    sign = 1 - 2 * (place % 2)
+
+    def width(i, reach):
+        return pl.ds(pl.multiple_of((sign * i + reach) * rows, rows), rows)
+
+    def toward(left, reach, u, terms):
+        value = None
+        for i in terms:
+            at = sign * i + 2 * SPAN + core
+            k = 2 + sign * (u - i)
+            if abs(u - i) == 2:
+                block = tri[at, k // 4]
+            else:
+                low = pl.multiple_of(2 * k * rows, rows)
+                block = jnp.concatenate(
+                    [buf[at, pl.ds(low, rows), :], buf[at, pl.ds(low + rows, rows), :]], axis=1
+                )
+            term = jnp.dot(left[:, width(i, reach)], block, preferred_element_type=jnp.float32)
+            value = term if value is None else value + term
+        return value
+
+    p_scale = 1.0 / math.sqrt(B)
+    t_scale = 1.0 / math.sqrt(B) / math.sqrt(2 * B)
+
+    def near_to(u, least, most):
+        return range(max(least, u - 2), min(most, u + 2) + 1)
+
+    def put_p(u, value):
+        p_low[:, width(u, 4)] = (value * p_scale).astype(p_low.dtype)
+
+    def put_t(u, value):
+        t_low[:, width(u, 6)] = (value * t_scale).astype(t_low.dtype)
+
+    for u in range(2, 5):
+        put_p(u, toward(row, 2, u, near_to(u, 0, 2)))
+    for u in range(-2, 2):
+        p_early[u + 2] = toward(row, 2, u, near_to(u, 0, 2))
+    for u in range(4, 7):
+        put_t(u, toward(p_low, 4, u, near_to(u, 2, 4)))
+    for u in range(0, 4):
+        t_early[u] = toward(p_low, 4, u, near_to(u, 2, 4))
+
     for j in chunks:
         take_pair(near, j)
-    for j in chunks[:4]:
-        take_pair(far, j)
+    for offset, j in FORWARDS[0]:
+        take_pair((far, x_far)[offset], j)
     unpack_own(near)
     unpack_other(near)
 
-    scale = 1.0 / math.sqrt(B)
-    for u in range(-4, 5):
-        p_low[:, (u + 4) * rows : (u + 5) * rows] = (
-            product(row, buf, tri, core, rows, 2, u, range(-2, 3)) * scale
-        ).astype(p_low.dtype)
-    for j in chunks[4:]:
-        take_pair(far, j)
-    scale = 1.0 / math.sqrt(B) / math.sqrt(2 * B)
-    for u in range(-6, 7):
-        t_low[:, (u + 6) * rows : (u + 7) * rows] = (
-            product(p_low, buf, tri, core, rows, 4, u, range(-4, 5)) * scale
-        ).astype(t_low.dtype)
-        for j in FORWARDS_T.get(u, ()):
-            take_pair(x_far, j)
+    for u in range(-4, 2):
+        value = toward(row, 2, u, near_to(u, -2, -1))
+        put_p(u, value + p_early[u + 2] if u >= -2 else value)
+    for offset, j in FORWARDS[1]:
+        take_pair((far, x_far)[offset], j)
+    for u in range(-6, 4):
+        value = toward(p_low, 4, u, near_to(u, -4, 1))
+        put_t(u, value + t_early[u] if u >= 0 else value)
+        for offset, j in FORWARDS_T.get(u, ()):
+            take_pair((far, x_far)[offset], j)
     for u in range(-6, 7):
         partial[:, (u + 6) * rows : (u + 7) * rows] = product(t_low, buf, tri, core, rows, 6, u, range(-4, 5))
-        for j in FORWARDS_OUT.get(u, ()):
-            take_pair(x_far, j)
+        for offset, j in FORWARDS_OUT.get(u, ()):
+            take_pair((far, x_far)[offset], j)
     for offset in (far, x_far):
         pltpu.make_async_copy(buf.at[center], buf.at[other(offset)], pair_recv.at[offset + SPAN]).wait()
     blocks = buf.at[pl.ds(0, SENT_BLOCKS)]
     remote(blocks, blocks, pair_recv.at[0], partner).wait_send()
+    relay.wait_send()
 
 
 def last_kernel(rows, t_low, partial, buf, out, tri, stage, out_sem):
@@ -295,9 +349,14 @@
             pltpu.VMEM((rows, 5 * rows), low),
             pltpu.VMEM((rows, 9 * rows), low),
             pltpu.VMEM((slots, 2, rows, rows), low),
+            pltpu.VMEM((CUTS[0], LANES), low),
+            pltpu.VMEM((4, rows, rows), jnp.float32),
+            pltpu.VMEM((4, rows, rows), jnp.float32),
+            pltpu.SemaphoreType.DMA,
             pltpu.SemaphoreType.DMA,
             pltpu.SemaphoreType.DMA((2 * SPAN, chunks)),
             pltpu.SemaphoreType.DMA((2 * SPAN + 1,)),
+            pltpu.SemaphoreType.DMA,
             pltpu.SemaphoreType.DMA((2, LOADS)),
         ],
         compiler_params=pltpu.CompilerParams(

time: 40.1 us -> 38.3 us (0.955); the launches traced: 39.6 us -> 38.2 us
  Pallas kernels: 39.6 us -> 38.2 us
    pallas_call x1, Pallas kernels: 37.4 us -> 36 us  [local(): pl.pallas_call(functools.partial(gather_kernel, n, rows), out_shape=(jax....]
where the time goes in v4:
time: 38.3 us; the launch traced here: 38.2 us
  Pallas kernels  38.2 us (100%)
    pallas_call x1, Pallas kernels, local(): pl.pallas_call(functools.partial(gather_kernel, n, rows), out_shape=(jax....  36 us
    pallas_call x1, Pallas kernels, local(): pl.pallas_call(functools.partial(last_kernel, rows), out_shape=jax.ShapeD...  2.14 us

profile of v4, /device:TPU:1, one launch (start us, length us, event | category | flops | bytes accessed | tf_op | source)
XLA Modules:
  0.0 38.2 jit_solution(5032936705627045162)
XLA Ops:
  0.0 36.0 %gather.1 = (bf16[256,3328]{1,0:T(8,128)(2,1)S(1)}, f32[256,3328]{1,0:T(8,128)S(1)}, bf16[14,2064,128]{2,1,0:T(8,128)(2,1)S(1)}) custom-call(s32[256,1280]{1,0:T(8,128)} %adjacency.1, bf16[256,1280]{1,0:T(8,128)(2,1)} %weight.1), custom_call_target="tpu_custom_call" | custom-call | tf_op jit(solution)/shard_map/gather/pallas_call | solution.py:337
  36.0 2.1 %last.1 = f32[256,4352]{1,0:T(8,128)} custom-call(bf16[256,3328]{1,0:T(8,128)(2,1)S(1)} %get-tuple-element.8.t_low, f32[256,3328]{1,0:T(8,128)S(1)} %get-tuple-element.9.partial, bf16[14,2064,128]{2,1,0:T(8,128)(2,1)S(1)} %get-tuple-element.10.buf), custom_call_target="tpu_custom_call" | custom-call | tf_op jit(solution)/shard_map/last/pallas_call | solution.py:367

commit v5 on v4

--- a/solution.py
+++ b/solution.py
@@ -16,16 +16,16 @@
 LANES = 128
 PAD = 16
 LOADS = 2
-CUTS = (256, 512, 768, 1024, 1280, 1536, 1792)
-LAG = 3
+CUTS = (256, 640, 1024, 1408, 1792)
+LAG = 2
 SENT_BLOCKS = 2 + 2 + 2 + (2 * SPAN + 1)
 FORWARDS = (
-    ((0, 0), (0, 1), (0, 2), (0, 3), (1, 1), (1, 2), (1, 3)),
-    ((0, 4), (0, 5), (0, 6), (0, 7), (1, 4)),
+    ((0, 0), (0, 1), (0, 2), (1, 1), (1, 2)),
+    ((0, 3), (0, 4), (0, 5), (1, 3)),
 )
-FORWARDS_T = {-3: ((1, 5),), 0: ((1, 6),), 3: ((1, 0), (1, 7))}
+FORWARDS_T = {-1: ((1, 4),), 3: ((1, 0), (1, 5))}
 FORWARDS_OUT = {}
-SPANS = ((-8, -5), (-5, -2), (3, 6), (6, 9))
+SPANS = ((-8, -5), (-5, -2), (3, 6), (6, 9), (-2, 1), (1, 3))
 
 
 def block_of(buf, tri, at, k, rows):
@@ -54,7 +54,7 @@
 
 
 def gather_kernel(
-    n, rows, adjacency, weight, t_low, partial, buf, adj, wgt, row, p_low, tri, via, p_early, t_early,
+    n, rows, adjacency, weight, t_low, partial, buf, tri, adj, wgt, row, p_low, via, p_early, t_early,
     send_sem, relay_sem, recv, pair_recv, via_recv, in_sem,
 ):
     me = lax.axis_index("blk")
@@ -261,7 +261,7 @@
     for u in range(2, 5):
         put_p(u, toward(row, 2, u, near_to(u, 0, 2)))
     for u in range(-2, 2):
-        p_early[u + 2] = toward(row, 2, u, near_to(u, 0, 2))
+        p_early[u + 3] = toward(row, 2, u, near_to(u, 0, 2))
     for u in range(4, 7):
         put_t(u, toward(p_low, 4, u, near_to(u, 2, 4)))
     for u in range(0, 4):
@@ -272,19 +272,29 @@
     for offset, j in FORWARDS[0]:
         take_pair((far, x_far)[offset], j)
     unpack_own(near)
+    put_p(-4, toward(row, 2, -4, (-2,)))
+    for u in range(-3, 1):
+        value = toward(row, 2, u, (-2,))
+        p_early[u + 3] = value + p_early[u + 3] if u > -3 else value
+    put_t(-6, toward(p_low, 4, -6, (-4,)))
+    for u in range(-5, -1):
+        t_early[u + 9] = toward(p_low, 4, u, (-4,))
     unpack_other(near)
 
-    for u in range(-4, 2):
-        value = toward(row, 2, u, near_to(u, -2, -1))
-        put_p(u, value + p_early[u + 2] if u >= -2 else value)
+    for u in range(-3, 2):
+        put_p(u, toward(row, 2, u, (-1,)) + p_early[u + 3])
     for offset, j in FORWARDS[1]:
         take_pair((far, x_far)[offset], j)
-    for u in range(-6, 4):
-        value = toward(p_low, 4, u, near_to(u, -4, 1))
-        put_t(u, value + t_early[u] if u >= 0 else value)
+    for u in range(-5, 4):
+        value = toward(p_low, 4, u, near_to(u, -3, 1))
+        if u <= -2:
+            value += t_early[u + 9]
+        elif u >= 0:
+            value += t_early[u]
+        put_t(u, value)
         for offset, j in FORWARDS_T.get(u, ()):
             take_pair((far, x_far)[offset], j)
-    for u in range(-6, 7):
+    for u in (*range(-6, -2), *range(3, 7)):
         partial[:, (u + 6) * rows : (u + 7) * rows] = product(t_low, buf, tri, core, rows, 6, u, range(-4, 5))
         for offset, j in FORWARDS_OUT.get(u, ()):
             take_pair((far, x_far)[offset], j)
@@ -295,22 +305,25 @@
     relay.wait_send()
 
 
-def last_kernel(rows, t_low, partial, buf, out, tri, stage, out_sem):
+def last_kernel(rows, t_low, partial, buf, tri, out, far_tri, stage, out_sem):
     core = lax.axis_index("blk") % CORES
     far = (-6, -5, 5, 6)
-    middle = pl.ds(6 * rows, 5 * rows)
-    writes = [pltpu.make_async_copy(partial.at[:, pl.ds(4 * rows, 5 * rows)], out.at[:, middle], out_sem.at[0])]
-    writes[0].start()
+    writes = []
     for i, m in enumerate(far):
-        tri[i, 0], tri[i, 1] = ends_of(buf, m + 2 * SPAN + core, rows)
+        far_tri[i, 0], far_tri[i, 1] = ends_of(buf, m + 2 * SPAN + core, rows)
     for low, high in SPANS:
         for u in range(low, high):
+            if abs(u) <= 2:
+                stage[:, (u + 8) * rows : (u + 9) * rows] = product(
+                    t_low, buf, tri, core, rows, 6, u, range(-4, 5)
+                )
+                continue
             terms = [(i, m) for i, m in enumerate(far) if abs(u - m) <= 2]
             right = []
             for i, m in terms:
                 k = u - m + 2
                 at = m + 2 * SPAN + core
-                right.append(tri[i, k // 4] if k in (0, 4) else block_of(buf, None, at, k, rows))
+                right.append(far_tri[i, k // 4] if k in (0, 4) else block_of(buf, None, at, k, rows))
             first, last = terms[0][1] + 6, terms[-1][1] + 6
             value = jnp.dot(
                 t_low[:, first * rows : (last + 1) * rows], jnp.concatenate(right, axis=0),
@@ -334,24 +347,24 @@
     chunks = len(CUTS) + 1
     vmem = pl.BlockSpec(memory_space=pltpu.VMEM)
     hbm = pl.BlockSpec(memory_space=pltpu.HBM)
-    t_low, partial, buf = pl.pallas_call(
+    t_low, partial, buf, tri = pl.pallas_call(
         functools.partial(gather_kernel, n, rows),
         out_shape=(
             jax.ShapeDtypeStruct((rows, 13 * rows), low),
             jax.ShapeDtypeStruct((rows, 13 * rows), jnp.float32),
             jax.ShapeDtypeStruct((slots, 8 * rows + PAD, LANES), low),
+            jax.ShapeDtypeStruct((slots, 2, rows, rows), low),
         ),
         in_specs=[hbm, hbm],
-        out_specs=(vmem, vmem, vmem),
+        out_specs=(vmem, vmem, vmem, vmem),
         scratch_shapes=[
             pltpu.VMEM(adjacency.shape, jnp.int32),
             pltpu.VMEM(weight.shape, low),
             pltpu.VMEM((rows, 5 * rows), low),
             pltpu.VMEM((rows, 9 * rows), low),
-            pltpu.VMEM((slots, 2, rows, rows), low),
             pltpu.VMEM((CUTS[0], LANES), low),
-            pltpu.VMEM((4, rows, rows), jnp.float32),
-            pltpu.VMEM((4, rows, rows), jnp.float32),
+            pltpu.VMEM((5, rows, rows), jnp.float32),
+            pltpu.VMEM((8, rows, rows), jnp.float32),
             pltpu.SemaphoreType.DMA,
             pltpu.SemaphoreType.DMA,
             pltpu.SemaphoreType.DMA((2 * SPAN, chunks)),
@@ -367,16 +380,16 @@
     return pl.pallas_call(
         functools.partial(last_kernel, rows),
         out_shape=jax.ShapeDtypeStruct((rows, 17 * rows), jnp.float32),
-        in_specs=[vmem, vmem, vmem],
+        in_specs=[vmem, vmem, vmem, vmem],
         out_specs=hbm,
         scratch_shapes=[
             pltpu.VMEM((4, 2, rows, rows), low),
             pltpu.VMEM((rows, 17 * rows), jnp.float32),
-            pltpu.SemaphoreType.DMA((len(SPANS) + 1,)),
+            pltpu.SemaphoreType.DMA((len(SPANS),)),
         ],
         compiler_params=pltpu.CompilerParams(vmem_limit_bytes=24 * 1024 * 1024),
         name="last",
-    )(t_low, partial, buf)
+    )(t_low, partial, buf, tri)
 
 
 def solution(mesh):

time: 38.3 us -> 37.6 us (0.982)
  Pallas kernels: 38.2 us -> 37.4 us
    pallas_call x1, Pallas kernels: 36 us -> 34.6 us  [local(): pl.pallas_call(functools.partial(gather_kernel, n, rows), out_shape=(jax....]
    pallas_call x1, Pallas kernels: 2.14 us -> 2.79 us  [local(): pl.pallas_call(functools.partial(last_kernel, rows), out_shape=jax.ShapeD...]
where the time goes in v5:
time: 37.6 us; the launch traced here: 37.4 us
  Pallas kernels  37.4 us (99%)
    pallas_call x1, Pallas kernels, local(): pl.pallas_call(functools.partial(gather_kernel, n, rows), out_shape=(jax....  34.6 us
    pallas_call x1, Pallas kernels, local(): pl.pallas_call(functools.partial(last_kernel, rows), out_shape=jax.ShapeD...  2.79 us

profile of v5, /device:TPU:1, one launch (start us, length us, event | category | flops | bytes accessed | tf_op | source)
XLA Modules:
  0.0 37.4 jit_solution(4464681762654584387)
XLA Ops:
  0.0 34.6 %gather.1 = (bf16[256,3328]{1,0:T(8,128)(2,1)S(1)}, f32[256,3328]{1,0:T(8,128)S(1)}, bf16[14,2064,128]{2,1,0:T(8,128)(2,1)S(1)}, bf16[14,2,256,256]{3,2,1,0:T(8,128)(2,1)S(1)}) custom-call(s32[256,1280]{1,0:T(8,128)} %adjacency.1, bf16[256,1280]{1,0:T(8,128)(2,1)} %weight.1), custom_call_target="tpu_custom_call" | custom-call | tf_op jit(solution)/shard_map/gather/pallas_call | solution.py:350
  34.6 2.8 %last.1 = f32[256,4352]{1,0:T(8,128)} custom-call(bf16[256,3328]{1,0:T(8,128)(2,1)S(1)} %get-tuple-element.9.t_low, f32[256,3328]{1,0:T(8,128)S(1)} %get-tuple-element.10.partial, bf16[14,2064,128]{2,1,0:T(8,128)(2,1)S(1)} %get-tuple-element.11.buf, bf16[14,2,256,256]{3,2,1,0:T(8,128)(2,1)S(1)} %get-tuple-element.12.tri), custom_call_target="tpu_custom_call" | custom-call | tf_op jit(solution)/shard_map/last/pallas_call | solution.py:380

commit v6 on v5

--- a/solution.py
+++ b/solution.py
@@ -17,7 +17,7 @@
 PAD = 16
 LOADS = 2
 CUTS = (256, 640, 1024, 1408, 1792)
-LAG = 2
+LAG = 3
 SENT_BLOCKS = 2 + 2 + 2 + (2 * SPAN + 1)
 FORWARDS = (
     ((0, 0), (0, 1), (0, 2), (1, 1), (1, 2)),

time: 37.6 us -> 37.6 us (level)
  no operation moved by 1% of the time
where the time goes in v6:
time: 37.6 us; the launch traced here: 37.4 us
  Pallas kernels  37.4 us (99%)
    pallas_call x1, Pallas kernels, local(): pl.pallas_call(functools.partial(gather_kernel, n, rows), out_shape=(jax....  34.6 us
    pallas_call x1, Pallas kernels, local(): pl.pallas_call(functools.partial(last_kernel, rows), out_shape=jax.ShapeD...  2.79 us

profile of v6, /device:TPU:1, one launch (start us, length us, event | category | flops | bytes accessed | tf_op | source)
XLA Modules:
  0.0 37.4 jit_solution(13850406328596058467)
XLA Ops:
  0.0 34.6 %gather.1 = (bf16[256,3328]{1,0:T(8,128)(2,1)S(1)}, f32[256,3328]{1,0:T(8,128)S(1)}, bf16[14,2064,128]{2,1,0:T(8,128)(2,1)S(1)}, bf16[14,2,256,256]{3,2,1,0:T(8,128)(2,1)S(1)}) custom-call(s32[256,1280]{1,0:T(8,128)} %adjacency.1, bf16[256,1280]{1,0:T(8,128)(2,1)} %weight.1), custom_call_target="tpu_custom_call" | custom-call | tf_op jit(solution)/shard_map/gather/pallas_call | solution.py:350
  34.6 2.8 %last.1 = f32[256,4352]{1,0:T(8,128)} custom-call(bf16[256,3328]{1,0:T(8,128)(2,1)S(1)} %get-tuple-element.9.t_low, f32[256,3328]{1,0:T(8,128)S(1)} %get-tuple-element.10.partial, bf16[14,2064,128]{2,1,0:T(8,128)(2,1)S(1)} %get-tuple-element.11.buf, bf16[14,2,256,256]{3,2,1,0:T(8,128)(2,1)S(1)} %get-tuple-element.12.tri), custom_call_target="tpu_custom_call" | custom-call | tf_op jit(solution)/shard_map/last/pallas_call | solution.py:380
